TPU v7x, 256 devices: a 8x8x2 block of a 8x8x16 slice. The times are simulated.
256 devices in a mesh: parts: 2 (over z), row: 128 (over y, x, core).
Axes of the slice: x: 8, y: 8, z: 2, core: 2. Of those that a mesh axis runs over, the one named last changes fastest.
The devices are a block of a 8x8x16 slice.
Arguments:
- sigma_top: bfloat16 [4096, 2048], P(('parts', 'row')), parts along dimension 0, may hold values from -2 to 8, as said below
- panel_par: bfloat16 [4096, 1024], P(('parts', 'row')), parts along dimension 0, may hold values from -0.25 to 0.25
- dinv_par: float32 [2048, 1024], P(('parts', 'row')), parts along dimension 0, may hold values from -2 to 8, as said below
- panel_kid_top: bfloat16 [4, 2048, 1024], P('parts', 'row'), parts along dimension 0, may hold values from -0.25 to 0.25
- panel_kid_par: bfloat16 [4, 1024, 1024], P('parts', 'row'), parts along dimension 0, may hold values from -0.375 to 0.375
- dvar_kid: float32 [4, 1024], P('parts'), parts along dimension 0, may hold values from 0.5 to 2
- mask_par: int32 [16, 4], P('parts'), parts along dimension 0, may hold values 0 or 1
- mask_kid_top: int32 [4, 8, 4], P('parts'), parts along dimension 0, may hold values 0 or 1
- mask_kid_par: int32 [4, 4, 4], P('parts'), parts along dimension 0, may hold values 0 or 1
Outputs:
- cross_par: bfloat16 [4096, 1024], P(('parts', 'row')), parts along dimension 0
- sigma_par: bfloat16 [2048, 1024], P(('parts', 'row')), parts along dimension 0
- cross_kid_top: bfloat16 [4, 2048, 1024], P('parts', 'row'), parts along dimension 0
- cross_kid_par: bfloat16 [4, 1024, 1024], P('parts', 'row'), parts along dimension 0
- variance_kid: float32 [4, 1024], P('parts'), parts along dimension 0
There are 2 independent parts, one for each index of `parts`. A program takes and returns all parts, laid end to end along the dimension named above; each array names one. Nothing has to cross between parts.
Inputs may be any that keep to these rules, and one draw needn't show every extreme that they name: `sigma_top`: symmetric positive definite. `dinv_par`: symmetric positive definite.
All inputs are finite; a program needn't handle non-finite values.
Results may differ from a plain program's by a relative error of at most 0.0052.
Values may be sent and summed in bfloat16 or wider, within the bound.
A program may use at most 64 MiB of HBM per device.

v0:
```python
import jax
import jax.numpy as jnp
from jax import lax
from jax.sharding import Mesh
from jax.sharding import PartitionSpec as P

BLK = 256
ROW = ("row_0", "row_1", "row_2")
PARTS_ROW = ("parts", "row_0", "row_1", "row_2")


def laid_out(tiles, dim):
    shape = list(tiles.shape[1:])
    shape[dim] *= tiles.shape[0]
    return jnp.moveaxis(tiles, 0, dim).reshape(shape)


def stacked_from(x, axes, order):
    tiles = x
    for k in order:
        tiles = lax.all_gather(tiles, axes[k])
    done = order[::-1]
    back = [done.index(k) for k in range(len(axes))]
    tiles = tiles.transpose(*back, *range(len(axes), tiles.ndim))
    return tiles.reshape(-1, *x.shape)


def gather_axes(x, axes, order, dim):
    return laid_out(stacked_from(x, axes, order), dim)


def sent_to_all(x, axis):
    copies = jnp.broadcast_to(x, (lax.axis_size(axis), *x.shape))
    return lax.all_to_all(copies, axis, split_axis=0, concat_axis=0, tiled=True)


def gathered_by_axis(x, axes, dim):
    far, near = axes
    leading = sent_to_all(x, far)
    tiles = jnp.swapaxes(sent_to_all(leading, near), 0, 1)
    return laid_out(tiles.reshape(-1, *x.shape), dim)


def over_copies(x, axis):
    return sent_to_all(x, axis).sum(axis=0)


def by_axis(x, axes):
    far, near = axes
    nearer = over_copies(x, near)
    return over_copies(nearer, far)


def block_mask(mask, rows, first):
    index = (first + jnp.arange(rows, dtype=jnp.int32)) // BLK
    picker = (index[:, None] == jnp.arange(mask.shape[-2], dtype=jnp.int32)[None, :]).astype(
        jnp.float32
    )
    picked = jnp.einsum("rb,...bc->...rc", picker, mask.astype(jnp.float32))
    return jnp.repeat(picked, BLK, axis=-1).astype(jnp.bfloat16)


def shards(
    sigma_top,
    panel_par,
    dinv_par,
    panel_kid_top,
    panel_kid_par,
    dvar_kid,
    mask_par,
    mask_kid_top,
    mask_kid_par,
):
    rows_top = sigma_top.shape[0]
    rows_par = dinv_par.shape[0]
    position = lax.axis_index(ROW)
    par_masked = panel_par * block_mask(mask_par, rows_top, position * rows_top)
    kid_top_masked = panel_kid_top * block_mask(mask_kid_top, rows_top, position * rows_top)
    kid_par_masked = panel_kid_par * block_mask(mask_kid_par, rows_par, position * rows_par)
    columns = sigma_top
    cross_wide = jnp.dot(
        columns, gather_axes(par_masked, ROW, (0, 1, 2), 0), preferred_element_type=jnp.float32
    )
    cross_par = cross_wide.astype(jnp.bfloat16)
    turned = lax.all_to_all(par_masked, ROW, split_axis=1, concat_axis=0, tiled=True)
    panel_rows = turned.T
    columns = panel_rows
    diag_sum = jnp.dot(
        columns,
        gathered_by_axis(cross_par, (("row_0", "row_1"), "row_2"), 0),
        preferred_element_type=jnp.float32,
    )
    sigma_par = (dinv_par + diag_sum).astype(jnp.bfloat16)
    turned_cross = lax.all_to_all(cross_par, ROW, split_axis=1, concat_axis=0, tiled=True)
    cross_rows_par = turned_cross.T
    piece = lax.all_gather(kid_top_masked, ROW, axis=1, tiled=True)
    upper = jnp.einsum("rc,kcw->krw", sigma_top, piece, preferred_element_type=jnp.float32)
    lower = jnp.einsum("rc,kcw->krw", cross_rows_par, piece, preferred_element_type=jnp.float32)
    acc_top = upper
    acc_par = lower
    piece = gathered_by_axis(kid_par_masked, (("row_0", "row_1"), "row_2"), 1)
    upper = acc_top + jnp.einsum(
        "rc,kcw->krw", cross_par, piece, preferred_element_type=jnp.float32
    )
    lower = acc_par + jnp.einsum(
        "rc,kcw->krw", sigma_par, piece, preferred_element_type=jnp.float32
    )
    cross_kid_top = upper.astype(jnp.bfloat16)
    cross_kid_par = lower.astype(jnp.bfloat16)
    partial_var = jnp.sum(
        kid_top_masked.astype(jnp.float32) * cross_kid_top.astype(jnp.float32), axis=1
    )
    partial_var = partial_var + jnp.sum(
        kid_par_masked.astype(jnp.float32) * cross_kid_par.astype(jnp.float32), axis=1
    )
    variance_kid = dvar_kid + by_axis(partial_var, (("row_0", "row_1"), "row_2"))
    return (cross_par, sigma_par, cross_kid_top, cross_kid_par, variance_kid)


def solution(mesh):
    finer = Mesh(
        mesh.devices.reshape(mesh.shape["parts"], 8, 8, 2), ("parts", "row_0", "row_1", "row_2")
    )
    return jax.shard_map(
        shards,
        mesh=finer,
        in_specs=(
            P(PARTS_ROW, None),
            P(PARTS_ROW, None),
            P(PARTS_ROW, None),
            P("parts", ROW, None),
            P("parts", ROW, None),
            P("parts", None),
            P("parts", None),
            P("parts", None, None),
            P("parts", None, None),
        ),
        out_specs=(
            P(PARTS_ROW, None),
            P(PARTS_ROW, None),
            P("parts", ROW, None),
            P("parts", ROW, None),
            P("parts", None),
        ),
        check_vma=False,
    )
```

profile of v0, /device:TPU:513, one launch (start us, length us, event | category | flops | bytes accessed | tf_op | source)
XLA Modules:
  0.0 339.7 jit_solution(4356895538441311231)
XLA Ops:
  7.2 0.0 copy-start
  7.2 0.1 all-gather.9.cloned.1.call-start
  7.3 0.8 convolution_convert_fusion.1
  8.1 0.1 copy.67
  8.2 0.1 broadcast_in_dim.33
  8.3 0.8 mul.31
  9.1 30.3 %all-gather = bf16[128,1024]{1,0:T(8,128)(2,1)} all-gather(bf16[16,1024]{1,0:T(8,128)(2,1)S(1)} %mul.31), channel_id=2, replica_groups=mesh['parts'=2,'row_0'=8,'row_1'=8,'row_2'=2] {'row_0'}, dimensions={0}, use_global_device_ids=true | all-gather | bytes 294912 | tf_op jit(solution)/shard_map/all_gather | solution.py:21
  39.3 0.1 all-gather.9.cloned.1.call-update
  39.4 0.1 all-gather.11.cloned.1.call-start
  39.5 53.2 %all-gather.9.cloned.1.call-done = bf16[64,16,1024]{2,1,0:T(8,128)(2,1)} async-done(((bf16[8,16,1024]{2,1,0:T(8,128)(2,1)}), bf16[64,16,1024]{2,1,0:T(8,128)(2,1)}) %all-gather.9.cloned.1.call-update) | async-done | bytes 2097168 | tf_op jit(solution)/shard_map/all_gather | solution.py:21
  92.7 0.1 all-gather.11.cloned.1.call-update
  92.7 0.1 all-gather.7.cloned.1.call-start
  92.8 0.7 convert_element_type.78
  93.5 0.1 fusion.21
  93.6 0.1 copy.72
  93.7 0.1 broadcast_in_dim.36
  93.9 1.5 mul.32
  95.4 0.1 all-gather.7.cloned.1.call-update
  95.4 0.7 convert_element_type.82
  96.1 0.1 copy.73
  96.2 0.1 fusion.25
  96.4 0.1 broadcast_in_dim.37
  96.4 0.8 mul.34
  97.2 1.6 broadcast_in_dim.38
  98.8 11.5 %all-to-all-start.3 = ((bf16[64,2,8,1024]{3,2,1,0:T(8,128)(2,1)}), bf16[64,2,8,1024]{3,2,1,0:T(8,128)(2,1)S(1)}, u32[]{:S(2)}, u32[]{:S(2)}) async-start(bf16[64,2,8,1024]{3,2,1,0:T(8,128)(2,1)} %broadcast_in_dim.38), calls=%async_computation.3 | async-start | bytes 4194304 | tf_op jit(solution)/shard_map/all_to_all | solution.py:34
  110.3 0.8 copy.69
  111.2 42.6 %all-to-all-done.3 = bf16[64,2,8,1024]{3,2,1,0:T(8,128)(2,1)S(1)} async-done(((bf16[64,2,8,1024]{3,2,1,0:T(8,128)(2,1)}), bf16[64,2,8,1024]{3,2,1,0:T(8,128)(2,1)S(1)}, u32[]{:S(2)}, u32[]{:S(2)}) %all-to-all-start.3) | async-done | bytes 2097184 | tf_op jit(solution)/shard_map/all_to_all | solution.py:34
  153.8 1.3 copy-done.4
  155.1 19.3 %all-to-all-start = ((bf16[16,128,8]{0,2,1:T(8,128)(2,1)}), bf16[16,128,8]{0,2,1:T(8,128)(2,1)S(1)}, u32[]{:S(2)}, u32[]{:S(2)}) async-start(bf16[16,128,8]{0,2,1:T(8,128)(2,1)} %bitcast.6), calls=%async_computation | async-start | bytes 524288 | tf_op jit(solution)/shard_map/all_to_all | solution.py:85
  174.4 1.8 copy.74
  176.2 0.0 all-gather.11.cloned.1.call-done
  176.2 2.6 copy.68
  178.8 0.0 copy-done
  178.9 0.7 convolution_convert_fusion
  179.5 0.2 copy.77
  179.7 8.8 %all-to-all-done = bf16[16,128,8]{0,2,1:T(8,128)(2,1)S(1)} async-done(((bf16[16,128,8]{0,2,1:T(8,128)(2,1)}), bf16[16,128,8]{0,2,1:T(8,128)(2,1)S(1)}, u32[]{:S(2)}, u32[]{:S(2)}) %all-to-all-start) | async-done | bytes 32800 | tf_op jit(solution)/shard_map/all_to_all | solution.py:85
  188.5 0.5 broadcast_in_dim.39
  189.0 8.9 %all_to_all.68 = bf16[2,64,2,8,1024]{4,3,1,2,0:T(8,128)(2,1)} all-to-all(bf16[2,64,2,8,1024]{4,3,1,2,0:T(8,128)(2,1)S(1)} %broadcast_in_dim.39), channel_id=1, replica_groups=mesh['parts'=2,'row_0'=8,'row_1'=8,'row_2'=2] {'row_2'}, dimensions={0} | all-to-all | bytes 8388608 | tf_op jit(solution)/shard_map/all_to_all | solution.py:34
  197.9 24.1 %all_to_all.69 = bf16[16,128,8]{0,2,1:T(8,128)(2,1)S(1)} all-to-all(bf16[16,128,8]{0,2,1:T(8,128)(2,1)S(1)} %bitcast.86), channel_id=1, replica_groups=mesh['parts'=2,'row_0'=8,'row_1'=8,'row_2'=2] {'row_0','row_1','row_2'}, dimensions={1} | all-to-all | bytes 65536 | tf_op jit(solution)/shard_map/all_to_all | solution.py:94
  222.0 1.6 broadcast_in_dim.34
  223.6 6.6 %all-to-all-start.1 = ((bf16[64,16,1024]{2,1,0:T(8,128)(2,1)}), bf16[64,16,1024]{2,1,0:T(8,128)(2,1)S(1)}, u32[]{:S(2)}, u32[]{:S(2)}) async-start(bf16[64,16,1024]{2,1,0:T(8,128)(2,1)} %broadcast_in_dim.34), calls=%async_computation.1 | async-start | bytes 4194304 | tf_op jit(solution)/shard_map/all_to_all | solution.py:34
  230.2 0.3 all_to_all.49
  230.5 2.6 copy.75
  233.1 0.0 copy-start.2
  233.1 1.9 copy-done.2
  235.1 0.7 fusion.2
  235.8 0.3 reshape.77
  236.1 44.0 %all-to-all-done.1 = bf16[64,16,1024]{2,1,0:T(8,128)(2,1)S(1)} async-done(((bf16[64,16,1024]{2,1,0:T(8,128)(2,1)}), bf16[64,16,1024]{2,1,0:T(8,128)(2,1)S(1)}, u32[]{:S(2)}, u32[]{:S(2)}) %all-to-all-start.1) | async-done | bytes 2097184 | tf_op jit(solution)/shard_map/all_to_all | solution.py:34
  280.1 0.5 broadcast_in_dim.35
  280.7 9.4 %all_to_all.70 = bf16[2,64,16,1024]{3,2,1,0:T(8,128)(2,1)S(1)} all-to-all(bf16[2,64,16,1024]{3,2,1,0:T(8,128)(2,1)S(1)} %broadcast_in_dim.35), channel_id=1, replica_groups=mesh['parts'=2,'row_0'=8,'row_1'=8,'row_2'=2] {'row_2'}, dimensions={0} | all-to-all | bytes 8388608 | tf_op jit(solution)/shard_map/all_to_all | solution.py:34
  290.1 0.8 copy.71
  290.9 0.7 fusion.17
  291.6 0.0 copy-start.3
  291.6 0.0 copy-start.1
  291.6 4.7 %fusion.27 = f32[2,1024,8]{1,2,0:T(8,128)S(1)} fusion(bf16[2,2048,1024]{2,1,0:T(8,128)(2,1)} %all-gather.7.cloned.1.call-done, bf16[2048,8,1]{0,1,2:T(8,128)(2,1)S(1)} %reshape.77), kind=kOutput, calls=%fused_computation.39 | convolution fusion | flops 67108864 | bytes 8486912 | tf_op jit(solution)/shard_map/rc,kcw->krw/dot_general | solution.py:98
  296.3 1.3 multiply_reduce_fusion.1
  297.6 1.0 copy-done.1
  298.6 0.0 copy-done.5
  298.7 1.8 multiply_reduce_fusion
  300.5 3.8 %all_to_all.71 = f32[2,2,1024]{2,1,0:T(2,128)S(1)} all-to-all(f32[2,2,1024]{2,1,0:T(2,128)S(1)} %broadcast_in_dim.40), channel_id=1, replica_groups=mesh['parts'=2,'row_0'=8,'row_1'=8,'row_2'=2] {'row_2'}, dimensions={0} | all-to-all | bytes 32768 | tf_op jit(solution)/shard_map/all_to_all | solution.py:34
  304.3 0.1 broadcast_in_dim.41
  304.5 27.9 %all_to_all.72 = f32[64,2,1024]{2,1,0:T(2,128)S(1)} all-to-all(f32[64,2,1024]{2,1,0:T(2,128)S(1)} %broadcast_in_dim.41), channel_id=1, replica_groups=mesh['parts'=2,'row_0'=8,'row_1'=8,'row_2'=2] {'row_0','row_1'}, dimensions={0} | all-to-all | bytes 1048576 | tf_op jit(solution)/shard_map/all_to_all | solution.py:34
  332.4 0.2 reduce_sum.39
  332.6 0.6 add.65
  (23 shorter events, 0.2 us)
Async XLA Ops:
  7.2 171.7 %copy-start = (bf16[16,2048]{1,0:T(8,128)(2,1)S(1)}, bf16[16,2048]{1,0:T(8,128)(2,1)}, u32[]{:S(2)}) copy-start(bf16[16,2048]{1,0:T(8,128)(2,1)} %param.9) | copy-start | bytes 196612
  7.2 85.5 %all-gather.9.cloned.1.call-start = ((), (), s32[]{:S(2)}) async-start(), calls=%async_computation.9 | async-start | bytes 2359296 | tf_op jit(solution)/shard_map/all_gather | solution.py:21
  39.4 136.8 %all-gather.11.cloned.1.call-start = ((), (), s32[]{:S(2)}) async-start(), calls=%async_computation.10 | async-start | bytes 6291456 | tf_op jit(solution)/shard_map/all_gather | solution.py:21
  92.7 198.8 %all-gather.7.cloned.1.call-start = ((), (), s32[]{:S(2)}) async-start(), calls=%async_computation.8 | async-start | bytes 8454144 | tf_op jit(solution)/shard_map/all_gather | solution.py:96
  98.8 55.0 %all-to-all-start.3 = ((bf16[64,2,8,1024]{3,2,1,0:T(8,128)(2,1)}), bf16[64,2,8,1024]{3,2,1,0:T(8,128)(2,1)S(1)}, u32[]{:S(2)}, u32[]{:S(2)}) async-start(bf16[64,2,8,1024]{3,2,1,0:T(8,128)(2,1)} %broadcast_in_dim.38), calls=%async_computation.3 | async-start | bytes 4194304 | tf_op jit(solution)/shard_map/all_to_all | solution.py:34
  153.8 1.3 copy-start.4
  155.1 33.4 %all-to-all-start = ((bf16[16,128,8]{0,2,1:T(8,128)(2,1)}), bf16[16,128,8]{0,2,1:T(8,128)(2,1)S(1)}, u32[]{:S(2)}, u32[]{:S(2)}) async-start(bf16[16,128,8]{0,2,1:T(8,128)(2,1)} %bitcast.6), calls=%async_computation | async-start | bytes 524288 | tf_op jit(solution)/shard_map/all_to_all | solution.py:85
  179.5 53.6 %copy-start.6 = (bf16[1024,16]{0,1:T(8,128)(2,1)}, bf16[1024,16]{0,1:T(8,128)(2,1)S(1)}, u32[]{:S(2)}) copy-start(bf16[1024,16]{0,1:T(8,128)(2,1)S(1)} %convolution_convert_fusion) | copy-start | bytes 98308
  223.6 56.6 %all-to-all-start.1 = ((bf16[64,16,1024]{2,1,0:T(8,128)(2,1)}), bf16[64,16,1024]{2,1,0:T(8,128)(2,1)S(1)}, u32[]{:S(2)}, u32[]{:S(2)}) async-start(bf16[64,16,1024]{2,1,0:T(8,128)(2,1)} %broadcast_in_dim.34), calls=%async_computation.1 | async-start | bytes 4194304 | tf_op jit(solution)/shard_map/all_to_all | solution.py:34
  233.1 2.0 copy-start.2
  290.1 0.8 copy-start.7
  291.6 4.7 %copy-start.8 = (bf16[8,1024]{1,0:T(8,128)(2,1)}, bf16[8,1024]{1,0:T(8,128)(2,1)S(1)}, u32[]{:S(2)}) copy-start(bf16[8,1024]{1,0:T(8,128)(2,1)S(1)} %fusion.17) | copy-start | bytes 49156
  291.6 4.7 %copy-start.3 = (bf16[2,64,2,8,1024]{4,3,2,0,1:T(8,128)(2,1)S(1)}, bf16[2,64,2,8,1024]{4,3,2,0,1:T(8,128)(2,1)}, u32[]{:S(2)}) copy-start(bf16[2,64,2,8,1024]{4,3,2,0,1:T(8,128)(2,1)} %copy-done.2) | copy-start | bytes 12582916
  291.6 7.1 %copy-start.1 = (bf16[2,2048,1024]{2,1,0:T(8,128)(2,1)S(1)}, bf16[2,2048,1024]{2,1,0:T(8,128)(2,1)}, u32[]{:S(2)}) copy-start(bf16[2,2048,1024]{2,1,0:T(8,128)(2,1)} %all-gather.7.cloned.1.call-done) | copy-start | bytes 25165828
  296.3 2.4 copy-start.5
  298.7 33.9 %copy-start.9 = (f32[2,1024]{1,0:T(2,128)S(1)}, f32[2,1024]{1,0:T(2,128)}, u32[]{:S(2)}) copy-start(f32[2,1024]{1,0:T(2,128)} %param.14) | copy-start | bytes 24580
Sparse Core Ops, SparseCore 0:
  39.5 53.1 all-gather.8
  94.5 24.7 all-gather.10
  122.5 108.7 all-gather.6
where the time goes:
time: 342 us; the launch traced here: 340 us
  waiting for transfers between devices  149 us (44%)
  blocking collectives  104 us (30%)
  starting transfers between devices  37.6 us (11%)
  local copies, waits for them, and re-layouts  18.9 us (6%)
  between operations  14 us (4%)
  matrix products  10.9 us (3%)
  other arithmetic  5.28 us (2%)
    all_to_all x2, waiting for transfers between devices, sent_to_all(): return lax.all_to_all(copies, axis, split_axis=0, concat_axis=0, tiled=True)  86.7 us
    all_gather x2, waiting for transfers between devices, stacked_from(): tiles = lax.all_gather(tiles, axes[k])  53.2 us
    all_to_all x4, blocking collectives, sent_to_all(): return lax.all_to_all(copies, axis, split_axis=0, concat_axis=0, tiled=True)  49.9 us
    all_gather x1, blocking collectives, stacked_from(): tiles = lax.all_gather(tiles, axes[k])  30.3 us
    all_to_all x1, blocking collectives, shards(): lax.all_to_all(cross_par, ROW, split_axis=1, concat_axis=0, tiled=True)  24.1 us
    all_to_all x1, starting transfers between devices, shards(): lax.all_to_all(par_masked, ROW, split_axis=1, concat_axis=0, tiled=True)  19.3 us
    all_to_all x2, starting transfers between devices, sent_to_all(): return lax.all_to_all(copies, axis, split_axis=0, concat_axis=0, tiled=True)  18.1 us
    all_to_all x1, waiting for transfers between devices, shards(): lax.all_to_all(par_masked, ROW, split_axis=1, concat_axis=0, tiled=True)  8.82 us
  transfers between devices with their start and end apart: 6, of which 4 were waited for; matrix products, arithmetic and copies ran while one was open for 6% of the time, Pallas kernels for 0%

commit v1 on v0

v1 whole, which is shorter than its diff:
```python
import functools

import jax
import jax.numpy as jnp
from jax import lax
from jax.experimental import pallas as pl
from jax.experimental.pallas import tpu as pltpu
from jax.sharding import Mesh
from jax.sharding import PartitionSpec as P

BLK = 256
N = 8
T = 128
ROW = ("row_0", "row_1", "row_2")
PARTS_ROW = ("parts", "row_0", "row_1", "row_2")
BF = jnp.bfloat16
F32 = jnp.float32

(
    QX,
    PX,
    PD,
    KX,
    SX,
    SD,
    DX,
    DD,
    QY,
    CY,
    WY,
    YY,
    VY,
    CE,
    CD,
    CO,
    GY,
    GO,
    XO,
    YO,
    VO,
) = range(21)


def cols(i):
    return pl.ds(pl.multiple_of(i * T, T), T)


def dot(a, b):
    return jnp.dot(a, b, preferred_element_type=F32)


def kernel(
    sig,
    par,
    dinv,
    ktop,
    kpar,
    dvar,
    m_par,
    m_top,
    m_kpar,
    c_out,
    s_out,
    x_out,
    y_out,
    v_out,
    pm,
    km,
    qm,
    db,
    pr,
    pt,
    sr,
    dr,
    kb,
    qf,
    pc,
    wf,
    w32,
    yp,
    yr,
    dq,
    cp,
    cx,
    cb,
    gp,
    gr,
    gs,
    go,
    xb,
    yb,
    vp,
    vr,
    vs,
    vo,
    send,
    recv,
):
    y, x, c = (lax.axis_index(a) for a in ROW)
    o = 1 - c
    slot = x * 2 + c

    def at(yy, xx, cc):
        return {"row_0": yy, "row_1": xx, "row_2": cc}

    def put(phase, src, dst, where):
        pltpu.make_async_remote_copy(
            src_ref=src,
            dst_ref=dst,
            send_sem=send.at[phase],
            recv_sem=recv.at[phase],
            device_id=where,
            device_id_type=pl.DeviceIdType.MESH,
        ).start()

    def take(phase, ref):
        pltpu.make_async_copy(ref, ref, recv.at[phase]).wait()

    def flush(phase, ref):
        pltpu.make_async_copy(ref, ref, send.at[phase]).wait()

    def others(f):
        @pl.loop(1, N)
        def _(d):
            f(d)

    def along_x(f):
        others(lambda d: f(lax.rem(x + d, N)))

    def along_y(f):
        others(lambda d: f(lax.rem(y + d, N)))

    def row(f):
        @pl.loop(1, 2 * N)
        def _(d):
            s = lax.rem(slot + d, 2 * N)
            f(s, s // 2, lax.rem(s, 2))

    barrier = pltpu.get_barrier_semaphore()

    def greet(where):
        pl.semaphore_signal(
            barrier, inc=1, device_id=where, device_id_type=pl.DeviceIdType.MESH
        )

    row(lambda s, xx, cc: greet(at(y, xx, cc)))
    along_y(lambda yy: greet(at(yy, x, c)))

    per = ktop.shape[2] // m_top.shape[2]
    for j in range(m_kpar.shape[2]):
        s = pl.ds(j * per, per)
        for k in range(2):
            qm[k, :, s] = kpar[k, :, s] * m_kpar[k, y // 2, j].astype(F32).astype(BF)
            km[k, :, s] = ktop[k, :, s] * m_top[k, y, j].astype(F32).astype(BF)
        pm[:, s] = par[:, s] * m_par[y, j].astype(F32).astype(BF)
    db[...] = dinv[...].astype(BF)
    qf[y, slot] = qm[c, :, cols(x)]
    kb[slot] = km[c, :, cols(x)]
    pr[x, c] = pm[...]
    sr[x, c] = sig[...]
    dr[x, c] = db[...]
    pl.semaphore_wait(barrier, 2 * N - 1 + N - 1)

    row(lambda s, xx, cc: put(QX, qm.at[cc, :, cols(xx)], qf.at[y, slot], at(y, xx, cc)))
    along_x(lambda xx: put(PX, pm, pr.at[x, c], at(y, xx, c)))
    row(lambda s, xx, cc: put(KX, km.at[cc, :, cols(xx)], kb.at[slot], at(y, xx, cc)))
    along_x(lambda xx: put(SX, sig, sr.at[x, c], at(y, xx, c)))
    along_x(lambda xx: put(DX, db, dr.at[x, c], at(y, xx, c)))

    take(QX, qf.at[0, pl.ds(0, 2 * N - 1)])
    along_y(lambda yy: put(QY, qf.at[y], qf.at[y], at(yy, x, c)))

    take(PX, pr.at[pl.ds(0, N - 1), 0])
    put(PD, pr.at[:, c], pr.at[:, c], at(y, x, o))
    take(PD, pr.at[:, 0])
    half = pl.ds(c * (N // 2), N // 2)
    pc[y] = pr[half, :, :, cols(x)].reshape(T, T)
    along_y(lambda yy: put(CY, pc.at[y], pc.at[y], at(yy, x, c)))
    p_rows = pr[...].reshape(2 * T, N * T)
    for j in range(N):
        turned = p_rows[:, j * T : (j + 1) * T].T
        pt[j] = turned.reshape(N, 2, 8, 2 * T)

    take(KX, kb.at[pl.ds(0, 2 * N - 1)])
    take(QY, qf.at[pl.ds(0, N - 1)])
    q_all = qf[...].reshape(N * T, T)
    w = kb[...].reshape(2 * T, T).astype(F32) + dot(p_rows, q_all)
    w32[...] = w
    wf[y] = w.astype(BF)
    along_y(lambda yy: put(WY, wf.at[y], wf.at[y], at(yy, x, c)))

    take(SX, sr.at[pl.ds(0, N - 1), 0])
    put(SD, sr.at[:, c], sr.at[:, c], at(y, x, o))
    take(DX, dr.at[pl.ds(0, N - 1), 0])
    put(DD, dr.at[:, c], dr.at[:, c], at(y, x, o))
    take(DD, dr.at[:, 0])
    dq[...] = dot(dr[...].reshape(T, N * T), qf[...].reshape(N * T, T))
    take(SD, sr.at[:, 0])
    take(CY, pc.at[pl.ds(0, N - 1)])
    acc = jnp.zeros((2 * T, T), F32)
    for j in range(N):
        part = sr[:, :, :, pl.ds(pl.multiple_of((2 * j + c) * T, T), T)]
        acc = acc + dot(part.reshape(2 * T, T), pc[j])
    cp[...] = acc.reshape(2, T, T)
    put(CE, cp.at[o], cx, at(y, x, o))
    take(CE, cx)
    cb[half] = (cp[c] + cx[...]).astype(BF).reshape(N // 2, 2, 16, T)
    put(CD, cb.at[half], cb.at[half], at(y, x, o))
    take(CD, cb.at[pl.ds(0, N // 2)])
    along_x(lambda xx: put(CO, cb.at[xx, c], c_out.at[:, cols(x)], at(y, xx, c)))
    c_out[:, cols(x)] = cb[x, c]
    gp[...] = (
        dot(pt[:, :, c].reshape(N * T // 2, 2 * T), cb[...].reshape(2 * T, T))
        .astype(BF)
        .reshape(N, T // 2, T)
    )
    along_y(lambda yy: put(GY, gp.at[yy], gr.at[y], at(yy, x, c)))
    gr[y] = gp[y]

    take(WY, wf.at[pl.ds(0, N - 1)])
    xs = dot(sr[...].reshape(2 * T, 2 * N * T), wf[...].reshape(2 * N * T, T))
    xb[...] = xs.astype(BF).reshape(2 * N, 16, T)
    yp[...] = (
        dot(pt[...].reshape(N * T, 2 * T), xb[...].reshape(2 * T, T))
        .astype(BF)
        .reshape(N, T, T)
    )
    along_y(lambda yy: put(YY, yp.at[yy], yr.at[y], at(yy, x, c)))
    yr[y] = yp[y]
    q_own = qf[y].reshape(T, T).astype(F32)
    v = jnp.sum(w32[...] * xs, axis=0, keepdims=True)
    v = v + jnp.sum(q_own * dq[...], axis=0, keepdims=True)
    vp[...] = v
    vr[y] = v
    along_y(lambda yy: put(VY, vp, vr.at[y], at(yy, x, c)))
    row(lambda s, xx, cc: put(XO, xb.at[s], x_out.at[c, :, cols(x)], at(y, xx, cc)))
    x_out[c, :, cols(x)] = xb[slot]

    take(GY, gr.at[pl.ds(0, N - 1)])
    g = gr[0].astype(F32)
    for j in range(1, N):
        g = g + gr[j].astype(F32)
    gs[...] = g.reshape(N, 8, T)
    along_x(lambda xx: put(GO, gs.at[xx], go.at[x], at(y, xx, c)))
    go[x] = gs[x]

    take(YY, yr.at[pl.ds(0, N - 1)])
    yy_sum = dq[...]
    for j in range(N):
        yy_sum = yy_sum + yr[j].astype(F32)
    yb[...] = yy_sum.astype(BF).reshape(2 * N, 8, T)
    row(lambda s, xx, cc: put(YO, yb.at[s], y_out.at[c, :, cols(x)], at(y, xx, cc)))
    y_out[c, :, cols(x)] = yb[slot]
    take(VY, vr.at[pl.ds(0, N - 1)])
    v = jnp.sum(vr[...], axis=0)
    vs[...] = v
    vo[slot] = v
    row(lambda s, xx, cc: put(VO, vs, vo.at[slot], at(y, xx, cc)))

    take(GO, go.at[pl.ds(0, N - 1)])
    for j in range(N):
        s = pl.ds(j * T, T)
        s_out[:, s] = (dinv[:, s] + go[j]).astype(BF)
    take(VO, vo.at[pl.ds(0, 2 * N - 1)])
    for j in range(N):
        s = pl.ds(j * T, T)
        for k in range(2):
            v_out[pl.ds(k, 1), s] = dvar[pl.ds(k, 1), s] + vo[2 * j + k]
    take(CO, kb.at[pl.ds(0, N - 1)])
    take(XO, kb.at[pl.ds(0, 2 * N - 1)])
    take(YO, qf.at[0, pl.ds(0, 2 * N - 1)])

    flush(QX, qf.at[0, pl.ds(0, 2 * N - 1)])
    flush(PX, pr.at[pl.ds(0, N - 1), 0])
    flush(PD, pr.at[:, 0])
    flush(KX, kb.at[pl.ds(0, 2 * N - 1)])
    flush(SX, sr.at[pl.ds(0, N - 1), 0])
    flush(SD, sr.at[:, 0])
    flush(DX, dr.at[pl.ds(0, N - 1), 0])
    flush(DD, dr.at[:, 0])
    flush(QY, qf.at[pl.ds(0, N - 1)])
    flush(CY, pc.at[pl.ds(0, N - 1)])
    flush(WY, wf.at[pl.ds(0, N - 1)])
    flush(YY, yr.at[pl.ds(0, N - 1)])
    flush(VY, vr.at[pl.ds(0, N - 1)])
    flush(CE, cx)
    flush(CD, cb.at[pl.ds(0, N // 2)])
    flush(CO, kb.at[pl.ds(0, N - 1)])
    flush(GY, gr.at[pl.ds(0, N - 1)])
    flush(GO, go.at[pl.ds(0, N - 1)])
    flush(XO, kb.at[pl.ds(0, 2 * N - 1)])
    flush(YO, qf.at[0, pl.ds(0, 2 * N - 1)])
    flush(VO, vo.at[pl.ds(0, 2 * N - 1)])


def shards(sig, par, dinv, ktop, kpar, dvar, m_par, m_top, m_kpar):
    vmem = pl.BlockSpec(memory_space=pltpu.VMEM)
    smem = pl.BlockSpec(memory_space=pltpu.SMEM)
    like = jax.ShapeDtypeStruct
    V = pltpu.VMEM
    return pl.pallas_call(
        kernel,
        name="selected_inverse",
        out_shape=(
            like(par.shape, BF),
            like(dinv.shape, BF),
            like(ktop.shape, BF),
            like(kpar.shape, BF),
            like(dvar.shape, F32),
        ),
        in_specs=[vmem] * 6 + [smem] * 3,
        out_specs=(vmem,) * 5,
        scratch_shapes=[
            V(par.shape, BF),
            V(ktop.shape, BF),
            V(kpar.shape, BF),
            V(dinv.shape, BF),
            V((N, 2, *par.shape), BF),
            V((N, N, 2, 8, 2 * T), BF),
            V((N, 2, *sig.shape), BF),
            V((N, 2, *dinv.shape), BF),
            V((2 * N, 16, T), BF),
            V((N, 2 * N, 8, T), BF),
            V((N, T, T), BF),
            V((N, 2 * T, T), BF),
            V((2 * T, T), F32),
            V((N, T, T), BF),
            V((N, T, T), BF),
            V((T, T), F32),
            V((2, T, T), F32),
            V((T, T), F32),
            V((N, 2, 16, T), BF),
            V((N, T // 2, T), BF),
            V((N, T // 2, T), BF),
            V((N, 8, T), F32),
            V((N, 8, T), F32),
            V((2 * N, 16, T), BF),
            V((2 * N, 8, T), BF),
            V((1, T), F32),
            V((N, 1, T), F32),
            V((1, T), F32),
            V((2 * N, 1, T), F32),
            pltpu.SemaphoreType.DMA((21,)),
            pltpu.SemaphoreType.DMA((21,)),
        ],
        compiler_params=pltpu.CompilerParams(collective_id=0, has_side_effects=True),
    )(sig, par, dinv, ktop, kpar, dvar, m_par, m_top, m_kpar)


def solution(mesh):
    finer = Mesh(
        mesh.devices.reshape(mesh.shape["parts"], N, N, 2), ("parts", "row_0", "row_1", "row_2")
    )
    return jax.shard_map(
        shards,
        mesh=finer,
        in_specs=(
            P(PARTS_ROW, None),
            P(PARTS_ROW, None),
            P(PARTS_ROW, None),
            P("parts", ROW, None),
            P("parts", ROW, None),
            P("parts", None),
            P("parts", None),
            P("parts", None, None),
            P("parts", None, None),
        ),
        out_specs=(
            P(PARTS_ROW, None),
            P(PARTS_ROW, None),
            P("parts", ROW, None),
            P("parts", ROW, None),
            P("parts", None),
        ),
        check_vma=False,
    )
```

time: 342 us -> 79 us (0.23)
  waiting for transfers between devices: 149 us -> 0 us
  blocking collectives: 104 us -> 0 us
  Pallas kernels: 0 us -> 71.1 us
  starting transfers between devices: 37.6 us -> 0 us
  between operations: 14 us -> 0.66 us
  local copies, waits for them, and re-layouts: 18.9 us -> 6.84 us
  matrix products: 10.9 us -> 0 us
  other arithmetic: 5.28 us -> 0 us
    all_to_all x3 -> x0, waiting for transfers between devices: 95.5 us -> none  [the longest x2 86.7 us: sent_to_all(): return lax.all_to_all(copies, axis, split_axis=0, concat_axis=0, tiled=True)]
    all_to_all x5 -> x0, blocking collectives: 74 us -> none  [the longest x4 49.9 us: sent_to_all(): return lax.all_to_all(copies, axis, split_axis=0, concat_axis=0, tiled=True)]
    pallas_call x0 -> x1, Pallas kernels: none -> 71.1 us  [shards(): pl.pallas_call(kernel, name='selected_inverse', out_shape=(like(par.shape...]
    all_gather x3 -> x0, waiting for transfers between devices: 53.2 us -> none  [the longest x2 53.2 us: stacked_from(): tiles = lax.all_gather(tiles, axes[k])]
    all_to_all x3 -> x0, starting transfers between devices: 37.4 us -> none  [the longest x1 19.3 us: shards(): lax.all_to_all(par_masked, ROW, split_axis=1, concat_axis=0, tiled=True)]
    all_gather x1 -> x0, blocking collectives: 30.3 us -> none  [stacked_from(): tiles = lax.all_gather(tiles, axes[k])]
    dot_general x7 -> x0, matrix products: 10.6 us -> none  [the longest x1 4.72 us: shards(): jnp.einsum('rc,kcw->krw', cross_rows_par, piece, preferred_element_type=j...]
    all_to_all x7 -> x0, local copies, waits for them, and re-layouts: 5.96 us -> none  [the longest x3 5.26 us: sent_to_all(): return lax.all_to_all(copies, axis, split_axis=0, concat_axis=0, tiled=True)]
  transfers between devices with their start and end apart: 6 -> 0, of which waited for: 4 -> 0; matrix products, arithmetic and copies ran while one was open for 6% -> 0% of each run, Pallas kernels for 0% -> 0%
where the time goes in v1:
time: 79 us; the launch traced here: 78.6 us
  Pallas kernels  71.1 us (90%)
  local copies, waits for them, and re-layouts  6.84 us (9%)
    pallas_call x1, Pallas kernels, shards(): pl.pallas_call(kernel, name='selected_inverse', out_shape=(like(par.shape...  71.1 us
    unnamed x15, local copies, waits for them, and re-layouts  6.84 us

profile of v1, /device:TPU:513, one launch (start us, length us, event | category | flops | bytes accessed | tf_op | source)
XLA Modules:
  0.0 78.6 jit_solution(7619765170597489983)
XLA Ops:
  0.6 0.0 copy-start.3
  0.6 1.4 %copy.14.m_par = s32[8,4]{1,0:T(8,128)} copy(s32[8,4]{0,1:T(4,128)} %param.15) | data formatting | bytes 256 | tf_op args[6]
  2.0 0.0 copy-done.3
  2.0 0.7 copy.15.m_top
  2.7 71.1 %selected_inverse.1 = (bf16[16,1024]{1,0:T(8,128)(2,1)}, bf16[8,1024]{1,0:T(8,128)(2,1)}, bf16[2,16,1024]{2,1,0:T(8,128)(2,1)}, bf16[2,8,1024]{2,1,0:T(8,128)(2,1)}, f32[2,1024]{1,0:T(2,128)}) custom-call(bf16[16,2048]{1,0:T(8,128)(2,1)} %sig.1, bf16[16,1024]{1,0:T(8,128)(2,1)} %par.1, f32[8,1024]{1,0:T(8,128)} %dinv.1, bf16[2,16,1024]{2,1,0:T(8,128)(2,1)} %ktop.1, ...), custom_call_target="tpu_custom_call" | custom-call | tf_op jit(solution)/shard_map/selected_inverse/pallas_call | solution.py:301
  73.8 0.0 copy-start
  73.8 1.4 %copy.21 = bf16[16,1024]{1,0:T(8,128)(2,1)} copy(bf16[16,1024]{1,0:T(8,128)(2,1)} %get-tuple-element.10) | data formatting | bytes 65536
  75.3 1.3 %copy.22 = bf16[8,1024]{1,0:T(8,128)(2,1)} copy(bf16[8,1024]{1,0:T(8,128)(2,1)} %get-tuple-element.11) | data formatting | bytes 32768
  76.6 0.0 copy-done
  76.6 0.0 copy-start.1
  76.6 0.6 copy.23
  77.2 0.1 copy-done.1
  77.3 0.0 copy-start.2
  77.3 0.6 copy.24
  78.0 0.1 copy-done.2
  78.0 0.6 copy.25
Async XLA Ops:
  0.6 1.4 %copy-start.3 = (s32[2,8,4]{1,2,0:T(4,128)S(1)}, s32[2,8,4]{1,2,0:T(4,128)}, u32[]{:S(2)}) copy-start(s32[2,8,4]{1,2,0:T(4,128)} %param.16) | copy-start | bytes 772
  73.8 2.7 %copy-start = (bf16[2,16,1024]{2,1,0:T(8,128)(2,1)S(1)}, bf16[2,16,1024]{2,1,0:T(8,128)(2,1)}, u32[]{:S(2)}) copy-start(bf16[2,16,1024]{2,1,0:T(8,128)(2,1)} %get-tuple-element.12) | copy-start | bytes 196612
  76.6 0.8 copy-start.1
  77.3 0.7 copy-start.2
